TPU v7x, 32 devices: a whole 2x2x4 slice. The times are simulated.
32 devices in a mesh: batch: 4 (over y, x), cols: 8 (over z, core).
Axes of the slice: x: 2, y: 2, z: 4, core: 2. Of those that a mesh axis runs over, the one named last changes fastest.
Arguments:
- grad_query: float32 [4, 2048, 2048], P('batch', None, 'cols'), may hold values from -0.875 to 0.875
- grad_key: float32 [4, 2048, 2048], P('batch', None, 'cols'), may hold values from -0.875 to 0.875
- grad_value: float32 [4, 2048, 2048], P('batch', None, 'cols'), may hold values from -0.875 to 0.875
- grad_mixed: float32 [4, 2048, 2048], P('batch', 'cols'), may hold values from -0.875 to 0.875
- grad_norm: float32 [4, 2048], P('batch'), may hold values from -8 to 8
- grad_bias: float32 [4, 2048], P('batch'), may hold values from -8 to 8
- weight_query: float32 [2048, 2048], P('batch', 'cols'), may hold values from -0.1875 to 0.1875
- weight_key: float32 [2048, 2048], P('batch', 'cols'), may hold values from -0.1875 to 0.1875
- weight_value: float32 [2048, 2048], P('batch', 'cols'), may hold values from -0.1875 to 0.1875
- weight_mixed: float32 [2048, 2048], P('cols', 'batch'), may hold values from -0.1875 to 0.1875
- weight_norm: float32 [2048], P('batch'), may hold values from 0.25 to 1.75
- weight_bias: float32 [2048], P('batch'), may hold values from -3 to 3
Outputs:
- copy_query: bfloat16 [2048, 2048], P(None, 'cols')
- copy_key: bfloat16 [2048, 2048], P(None, 'cols')
- copy_value: bfloat16 [2048, 2048], P(None, 'cols')
- copy_mixed: bfloat16 [2048, 2048], P('cols')
- copy_norm: bfloat16 [2048], replicated
- copy_bias: bfloat16 [2048], replicated
- new_query: float32 [2048, 2048], P('batch', 'cols')
- new_key: float32 [2048, 2048], P('batch', 'cols')
- new_value: float32 [2048, 2048], P('batch', 'cols')
- new_mixed: float32 [2048, 2048], P('cols', 'batch')
- new_norm: float32 [2048], P('batch')
- new_bias: float32 [2048], P('batch')
All inputs are finite; a program needn't handle non-finite values.
Results may differ from a plain program's by a relative error of at most 0.0004.
Values may be sent and summed in bfloat16 or wider, within the bound.
A program may use at most 64 MiB of HBM per device.

v0:
```python
import functools
import math

import jax
import jax.numpy as jnp
from jax import lax
from jax.experimental import pallas as pl
from jax.experimental.pallas import tpu as pltpu
from jax.sharding import PartitionSpec as P

learn_rate = 0.4
LANES = 128
ORDER = (
    ("F0", "F1", "S", "W0", "W1", "W2", "W3", "A0", "F2", "A1", "F3", "N", "B0")
    + ("A2", "B1", "U0", "A3", "B2", "U1", "P0", "B3", "U2", "P1", "U3", "P2", "P3")
)


def kernel(n, m, n_x, n_y, *refs):
    grads, small_grads = refs[0:4], refs[4:6]
    weights, small_weights = refs[6:10], refs[10:12]
    copies, news = refs[12:16], refs[16:20]
    small_full, small_own = refs[20:22]
    scratch = refs[22:]
    first_in, second_in, held = scratch[0:4], scratch[4:8], scratch[8:12]
    total, own_weight = scratch[12:16], scratch[16:20]
    squares, squares_in, small_in = scratch[20:23]
    (
        load_sem, weight_sem,
        first_send, first_recv, second_send, second_recv,
        square_send, square_recv, square_own,
        back_send, back_recv, spread_send, spread_recv,
        small_send, small_recv, small_local,
    ) = scratch[23:]
    rate = n ** (-0.5)

    me = lax.axis_index("batch")
    col = lax.axis_index("cols")
    y, x = me // n_x, lax.rem(me, n_x)

    def spot(half, d_first, d_second):
        if half == 0:
            return lax.rem(y + d_second, n_y) * n_x + lax.rem(x + d_first, n_x)
        return lax.rem(y + d_first, n_y) * n_x + lax.rem(x + d_second, n_x)

    def extents(half):
        return (n_x, n_y) if half == 0 else (n_y, n_x)

    def piece(a, ref, chunk, half):
        rows, columns = total[a].shape
        depth = rows // 2
        if a < 3:
            start = pl.multiple_of(chunk * rows + half * depth, depth)
            return ref.at[pl.ds(start, depth), :]
        start = pl.multiple_of(chunk * columns, columns)
        return ref.at[pl.ds(half * depth, depth), pl.ds(start, columns)]

    loads, weight_loads = {}, []
    for a in range(4):
        for half in range(2):
            for d in range(extents(half)[1]):
                loads[a, half, d] = pltpu.make_async_copy(
                    piece(a, grads[a].at[0], spot(half, 0, d), half),
                    held[a].at[half, d],
                    load_sem.at[a, half, d],
                )
        weight_loads.append(pltpu.make_async_copy(weights[a], own_weight[a], weight_sem.at[a]))
    small_loads, width = [], small_weights[0].shape[1]
    for i in range(2):
        small_loads.append(
            pltpu.make_async_copy(small_grads[i], small_in.at[me, :, pl.ds(i * n * width, n * width)], small_local.at[i])
        )
        small_loads.append(
            pltpu.make_async_copy(
                small_weights[i], small_in.at[me, :, pl.ds((2 * n + i) * width, width)], small_local.at[2 + i]
            )
        )

    barrier = pltpu.get_barrier_semaphore()
    for d in range(1, n):
        pl.semaphore_signal(barrier, inc=1, device_id={"batch": lax.rem(me + d, n)})
    for d in range(1, m):
        pl.semaphore_signal(barrier, inc=1, device_id={"cols": lax.rem(col + d, m)})
    for copy in small_loads:
        copy.start()
    for copy in weight_loads:
        copy.start()
    for copy in loads.values():
        copy.start()
    pl.semaphore_wait(barrier, n - 1 + m - 1)

    first, small = {}, []

    def send_first(a):
        for d_second in range(max(n_x, n_y) - 1, -1, -1):
            for half in range(2):
                n_first, n_second = extents(half)
                if d_second >= n_second:
                    continue
                for d_first in range(1, n_first):
                    copy = pltpu.make_async_remote_copy(
                        src_ref=piece(a, grads[a].at[0], spot(half, d_first, d_second), half),
                        dst_ref=first_in[a].at[half, d_first - 1, d_second],
                        send_sem=first_send.at[a, half, d_first - 1, d_second],
                        recv_sem=first_recv.at[a, half, d_first - 1, d_second],
                        device_id={"batch": spot(half, d_first, 0)},
                    )
                    copy.start()
                    first[a, half, d_first, d_second] = copy

    def send_small():
        for copy in small_loads:
            copy.wait()
        for d in range(1, n):
            copy = pltpu.make_async_remote_copy(
                src_ref=small_in.at[me],
                dst_ref=small_in.at[me],
                send_sem=small_send.at[d - 1],
                recv_sem=small_recv.at[d - 1],
                device_id={"batch": lax.rem(me + d, n)},
            )
            copy.start()
            small.append(copy)

    def row_squares(a, value):
        value = value * value
        if a == 3:
            return jnp.sum(value, axis=0, keepdims=True)
        folded = value[:, :LANES]
        for start in range(LANES, value.shape[1], LANES):
            folded = folded + value[:, start : start + LANES]
        return jnp.sum(folded.T, axis=0, keepdims=True)

    def weigh(a):
        weight_loads[a].wait()
        squares[a, 0:1] = row_squares(a, own_weight[a][...])

    second = {}

    def add_first(a):
        for d_second in range(max(n_x, n_y) - 1, -1, -1):
            for half in range(2):
                n_first, n_second = extents(half)
                if d_second >= n_second:
                    continue
                loads[a, half, d_second].wait()
                value = held[a][half, d_second]
                for d_first in range(1, n_first):
                    first[a, half, d_first, d_second].wait_recv()
                    value = value + first_in[a][half, d_first - 1, d_second]
                held[a][half, d_second] = value
                if d_second > 0:
                    copy = pltpu.make_async_remote_copy(
                        src_ref=held[a].at[half, d_second],
                        dst_ref=second_in[a].at[half, d_second - 1],
                        send_sem=second_send.at[a, half, d_second - 1],
                        recv_sem=second_recv.at[a, half, d_second - 1],
                        device_id={"batch": spot(half, 0, d_second)},
                    )
                    copy.start()
                    second[a, half, d_second] = copy

    exchange = {}

    def add_second(a):
        depth = total[a].shape[0] // 2
        for half in range(2):
            value = held[a][half, 0]
            for d_second in range(1, extents(half)[1]):
                second[a, half, d_second].wait_recv()
                value = value + second_in[a][half, d_second - 1]
            total[a][half * depth : (half + 1) * depth] = value * rate
        squares[a, 1:2] = row_squares(a, total[a][...])
        own = pltpu.make_async_copy(squares.at[a], squares_in.at[a, col], square_own.at[a])
        exchange[a] = [own]
        for d in range(1, m):
            copy = pltpu.make_async_remote_copy(
                src_ref=squares.at[a],
                dst_ref=squares_in.at[a, col],
                send_sem=square_send.at[a, d - 1],
                recv_sem=square_recv.at[a, d - 1],
                device_id={"cols": lax.rem(col + d, m)},
            )
            copy.start()
            exchange[a].append(copy)
        own.start()

    back, spread = {}, {}

    def send_spread(a, half, d_second):
        n_first, n_second = extents(half)
        slab = piece(a, copies[a], spot(half, 0, n_second - d_second), half)
        for d_first in range(1, n_first):
            copy = pltpu.make_async_remote_copy(
                src_ref=slab,
                dst_ref=slab,
                send_sem=spread_send.at[a, half, d_first - 1, d_second],
                recv_sem=spread_recv.at[a, half, d_first - 1, d_second],
                device_id={"batch": spot(half, d_first, 0)},
            )
            copy.start()
            spread[a, half, d_first, d_second] = copy

    def update(a):
        exchange[a][0].wait()
        for copy in exchange[a][1:]:
            copy.wait_recv()
        both = squares_in[a, 0]
        for d in range(1, m):
            both = both + squares_in[a, d]
        ratio = learn_rate * (jnp.sqrt(both[0:1]) * lax.rsqrt(both[1:2] + 1e-06))
        rows, columns = total[a].shape
        if a < 3:
            ratio = jnp.broadcast_to(ratio, (LANES, rows)).T
            for start in range(0, columns, LANES):
                block = slice(start, start + LANES)
                news[a][:, block] = own_weight[a][:, block] - total[a][:, block] * ratio
        else:
            news[a][...] = own_weight[a][...] - total[a][...] * ratio
        depth = rows // 2
        for half in range(2):
            piece(a, copies[a], me, half)[...] = news[a][half * depth : (half + 1) * depth].astype(jnp.bfloat16)
        for half in range(2):
            slab = piece(a, copies[a], me, half)
            for d_second in range(1, extents(half)[1]):
                copy = pltpu.make_async_remote_copy(
                    src_ref=slab,
                    dst_ref=slab,
                    send_sem=back_send.at[a, half, d_second - 1],
                    recv_sem=back_recv.at[a, half, d_second - 1],
                    device_id={"batch": spot(half, 0, d_second)},
                )
                copy.start()
                back[a, half, d_second] = copy
            send_spread(a, half, 0)

    def pass_on(a):
        for half in range(2):
            for d_second in range(1, extents(half)[1]):
                back[a, half, d_second].wait_recv()
                send_spread(a, half, d_second)

    def update_small():
        for copy in small:
            copy.wait()
        for i in range(2):
            value = small_in[0, :, i * n * width : (i + 1) * n * width]
            for j in range(1, n):
                value = value + small_in[j, :, i * n * width : (i + 1) * n * width]
            value = value * rate
            for j in range(n):
                weight = small_in[j, :, (2 * n + i) * width : (2 * n + i + 1) * width]
                small_full[i, j] = weight - learn_rate * value[:, j * width : (j + 1) * width]
            small_own[i] = small_full[i, me]

    steps = dict(
        F=send_first, S=send_small, W=weigh, A=add_first, N=update_small, B=add_second, U=update, P=pass_on
    )
    for step in ORDER:
        steps[step[0]](*map(int, step[1:]))
    for copies_sent in (first, second, back, spread):
        for copy in copies_sent.values():
            copy.wait_send()
    for a in range(4):
        for copy in exchange[a][1:]:
            copy.wait_send()
    for copy in spread.values():
        copy.wait_recv()


def finish(n, *refs):
    results, full, own = refs[0:8], refs[8], refs[9]
    outs, small_copies, small_news = refs[10:18], refs[18:20], refs[20:22]
    copy_rows, new_rows, sem, small_sem = refs[22:24], refs[24:26], refs[26], refs[27]
    moves = [pltpu.make_async_copy(results[i], outs[i], sem.at[i]) for i in range(8)]
    for move in moves:
        move.start()
    width = full.shape[-1]
    for i in range(2):
        for j in range(n):
            copy_rows[i][j * width : (j + 1) * width] = full[i, j, 0].astype(jnp.bfloat16)
        new_rows[i][...] = own[i, 0]
    for i in range(2):
        moves.append(pltpu.make_async_copy(copy_rows[i], small_copies[i], small_sem.at[i]))
        moves.append(pltpu.make_async_copy(new_rows[i], small_news[i], small_sem.at[2 + i]))
    for move in moves[8:]:
        move.start()
    for move in moves:
        move.wait()


def solution(mesh):
    n, m = mesh.shape["batch"], mesh.shape["cols"]
    n_x = math.isqrt(n)
    if n_x * n_x != n:
        n_x = n
    n_y = n // n_x
    most = max(n_x, n_y)

    def per_device(*args):
        args = args[:10] + tuple(w.reshape(1, -1) for w in args[10:])
        grads, weights, width = args[0:4], args[6:10], args[10].shape[1]
        blocks = [w.shape for w in weights]
        slices = blocks[0][0]
        slabs = [(b[0] // 2, b[1]) for b in blocks]
        f32, bf16 = jnp.float32, jnp.bfloat16
        DMA = pltpu.SemaphoreType.DMA
        hops = max(most - 1, 1)
        hbm = pl.BlockSpec(memory_space=pltpu.HBM)
        vmem = pl.BlockSpec(memory_space=pltpu.VMEM)
        out_shape = (
            [jax.ShapeDtypeStruct(g.shape[1:], bf16) for g in grads]
            + [jax.ShapeDtypeStruct(b, f32) for b in blocks]
            + [jax.ShapeDtypeStruct((2, n, 1, width), f32), jax.ShapeDtypeStruct((2, 1, width), f32)]
        )
        results = pl.pallas_call(
            functools.partial(kernel, n, m, n_x, n_y),
            out_shape=[pltpu.VMEM(o.shape, o.dtype) for o in out_shape],
            in_specs=[hbm] * 12,
            out_specs=[vmem] * 10,
            scratch_shapes=(
                [pltpu.VMEM((2, hops, most) + s, f32) for s in slabs]
                + [pltpu.VMEM((2, hops) + s, f32) for s in slabs]
                + [pltpu.VMEM((2, most) + s, f32) for s in slabs]
                + [pltpu.VMEM(b, f32) for b in blocks]
                + [pltpu.VMEM(b, f32) for b in blocks]
                + [
                    pltpu.VMEM((4, 2, slices), f32),
                    pltpu.VMEM((4, m, 2, slices), f32),
                    pltpu.VMEM((n, 1, 2 * (n + 1) * width), f32),
                    DMA((4, 2, most)),
                    DMA((4,)),
                    DMA((4, 2, hops, most)),
                    DMA((4, 2, hops, most)),
                    DMA((4, 2, hops)),
                    DMA((4, 2, hops)),
                    DMA((4, m)),
                    DMA((4, m)),
                    DMA((4,)),
                    DMA((4, 2, hops)),
                    DMA((4, 2, hops)),
                    DMA((4, 2, hops, most)),
                    DMA((4, 2, hops, most)),
                    DMA((n,)),
                    DMA((n,)),
                    DMA((4,)),
                ]
            ),
            compiler_params=pltpu.CompilerParams(
                collective_id=0, has_side_effects=True, vmem_limit_bytes=40 * 2**20
            ),
        )(*[pltpu.with_memory_space_constraint(v, pltpu.HBM) for v in args])
        done = pl.pallas_call(
            functools.partial(finish, n),
            out_shape=out_shape[:8]
            + [jax.ShapeDtypeStruct((n * width,), bf16)] * 2
            + [jax.ShapeDtypeStruct((width,), f32)] * 2,
            in_specs=[vmem] * 10,
            out_specs=[hbm] * 12,
            scratch_shapes=[pltpu.VMEM((n * width,), bf16)] * 2
            + [pltpu.VMEM((width,), f32)] * 2
            + [DMA((8,)), DMA((4,))],
            compiler_params=pltpu.CompilerParams(vmem_limit_bytes=2**20),
        )(*results)
        return tuple(done[0:4]) + tuple(done[8:10]) + tuple(done[4:8]) + tuple(done[10:12])

    in_specs = (
        (P("batch", None, "cols"),) * 3
        + (P("batch", "cols", None),)
        + (P("batch", None),) * 2
        + (P("batch", "cols"),) * 3
        + (P("cols", "batch"),)
        + (P("batch"),) * 2
    )
    out_specs = (
        (P(None, "cols"),) * 3
        + (P("cols", None),)
        + (P(),) * 2
        + (P("batch", "cols"),) * 3
        + (P("cols", "batch"),)
        + (P("batch"),) * 2
    )
    return jax.shard_map(per_device, mesh=mesh, in_specs=in_specs, out_specs=out_specs, check_vma=False)
```

profile of v0, /device:TPU:0, one launch (start us, length us, event | category | flops | bytes accessed | tf_op | source)
XLA Modules:
  0.0 115.1 jit_solution(6842031095926527369)
XLA Ops:
  0.6 111.6 %shard_map.211 = (bf16[2048,256]{1,0:T(8,128)(2,1)S(1)}, bf16[2048,256]{1,0:T(8,128)(2,1)S(1)}, bf16[2048,256]{1,0:T(8,128)(2,1)S(1)}, bf16[256,2048]{1,0:T(8,12...) custom-call(f32[1,2048,256]{2,1,0:T(8,128)} %refs_0_.1, ...), custom_call_target="tpu_custom_call" | custom-call | tf_op jit(solution)/shard_map/pallas_call | solution.py:316
  112.3 2.8 %shard_map.212 = (bf16[2048,256]{1,0:T(8,128)(2,1)}, bf16[2048,256]{1,0:T(8,128)(2,1)}, bf16[2048,256]{1,0:T(8,128)(2,1)}, bf16[256,2048]{1,0:T(8,128)(2,1)}, f3...) custom-call(bf16[2048,256]{1,0:T(8,128)(2,1)S(1)} %get-tuple-element, ...), custom_call_target="tpu_custom_call" | custom-call | tf_op jit(solution)/shard_map/pallas_call | solution.py:353
where the time goes:
time: 115 us
  Pallas kernels  114 us (99%)
    pallas_call x1, Pallas kernels, per_device(): pl.pallas_call(functools.partial(kernel, n, m, n_x, n_y), out_shape=[pltp...  112 us
    pallas_call x1, Pallas kernels, per_device(): pl.pallas_call(functools.partial(finish, n), out_shape=out_shape[:8] + [j...  2.78 us

commit v1 on v0

--- a/solution.py
+++ b/solution.py
@@ -10,6 +10,7 @@
 
 learn_rate = 0.4
 LANES = 128
+LOW, SPAN, TINY = 87.0, 175.0, 1e-30
 ORDER = (
     ("F0", "F1", "S", "W0", "W1", "W2", "W3", "A0", "F2", "A1", "F3", "N", "B0")
     + ("A2", "B1", "U0", "A3", "B2", "U1", "P0", "B3", "U2", "P1", "U3", "P2", "P3")
@@ -24,14 +25,18 @@
     scratch = refs[22:]
     first_in, second_in, held = scratch[0:4], scratch[4:8], scratch[8:12]
     total, own_weight = scratch[12:16], scratch[16:20]
-    squares, squares_in, small_in = scratch[20:23]
+    raw, first_out, second_out = scratch[20:24], scratch[24:28], scratch[28:32]
+    first_unit, first_unit_in = scratch[32:36], scratch[36:40]
+    second_unit, second_unit_in = scratch[40:44], scratch[44:48]
+    squares, squares_in, small_in = scratch[48:51]
     (
-        load_sem, weight_sem,
+        load_sem, raw_sem, weight_sem,
         first_send, first_recv, second_send, second_recv,
+        first_unit_send, first_unit_recv, second_unit_send, second_unit_recv,
         square_send, square_recv, square_own,
         back_send, back_recv, spread_send, spread_recv,
         small_send, small_recv, small_local,
-    ) = scratch[23:]
+    ) = scratch[51:]
     rate = n ** (-0.5)
 
     me = lax.axis_index("batch")
@@ -55,10 +60,19 @@
         start = pl.multiple_of(chunk * columns, columns)
         return ref.at[pl.ds(half * depth, depth), pl.ds(start, columns)]
 
-    loads, weight_loads = {}, []
+    loads, raw_loads, weight_loads = {}, {}, []
     for a in range(4):
-        for half in range(2):
-            for d in range(extents(half)[1]):
+        for d in range(max(n_x, n_y) - 1, -1, -1):
+            for half in range(2):
+                n_first, n_second = extents(half)
+                if d >= n_second:
+                    continue
+                for d_first in range(1, n_first):
+                    raw_loads[a, half, d_first, d] = pltpu.make_async_copy(
+                        piece(a, grads[a].at[0], spot(half, d_first, d), half),
+                        raw[a].at[half, d_first - 1, d],
+                        raw_sem.at[a, half, d_first - 1, d],
+                    )
                 loads[a, half, d] = pltpu.make_async_copy(
                     piece(a, grads[a].at[0], spot(half, 0, d), half),
                     held[a].at[half, d],
@@ -81,32 +95,105 @@
         pl.semaphore_signal(barrier, inc=1, device_id={"batch": lax.rem(me + d, n)})
     for d in range(1, m):
         pl.semaphore_signal(barrier, inc=1, device_id={"cols": lax.rem(col + d, m)})
+    for key, copy in raw_loads.items():
+        if key[0] == 0:
+            copy.start()
     for copy in small_loads:
         copy.start()
+    for key, copy in raw_loads.items():
+        if key[0] == 1:
+            copy.start()
+    for key, copy in loads.items():
+        if key[0] < 2:
+            copy.start()
     for copy in weight_loads:
         copy.start()
-    for copy in loads.values():
-        copy.start()
-    pl.semaphore_wait(barrier, n - 1 + m - 1)
+    for key, copy in raw_loads.items():
+        if key[0] > 1:
+            copy.start()
+    for key, copy in loads.items():
+        if key[0] > 1:
+            copy.start()
+
+    def across(a, line, depth):
+        if a < 3:
+            return jnp.broadcast_to(line, (LANES, depth)).T
+        return line
+
+    def blocks_of(a, columns):
+        if a < 3:
+            return [slice(start, start + LANES) for start in range(0, columns, LANES)]
+        return [slice(0, columns)]
+
+    def encode(a, source, code, unit):
+        depth, columns = source.shape
+        value = source[...]
+        size = jnp.abs(value)
+        if a < 3:
+            folded = functools.reduce(jnp.maximum, [size[:, block] for block in blocks_of(a, columns)])
+            size = folded.T
+        most = jnp.maximum(jnp.max(size, axis=0, keepdims=True), TINY)
+        unit[...] = most * SPAN**-2
+        gain = across(a, SPAN**2 / most, depth)
+        for block in blocks_of(a, columns):
+            part = value[:, block]
+            spread_out = jnp.abs(part) * gain
+            level = jnp.exp(spread_out * lax.rsqrt(spread_out + TINY) - LOW)
+            code[:, block] = jnp.where(part < 0, -level, level).astype(jnp.bfloat16)
+
+    def decode(a, code, unit):
+        depth, columns = code.shape
+        scale = across(a, unit[...], depth)
+        parts = []
+        for block in blocks_of(a, columns):
+            part = code[:, block].astype(jnp.float32)
+            root = jnp.log(jnp.abs(part)) + LOW
+            level = root * root * scale
+            parts.append(jnp.where(part < 0, -level, level))
+        return jnp.concatenate(parts, axis=1) if len(parts) > 1 else parts[0]
 
     first, small = {}, []
+    entered = []
 
     def send_first(a):
         for d_second in range(max(n_x, n_y) - 1, -1, -1):
+            ready = []
             for half in range(2):
                 n_first, n_second = extents(half)
                 if d_second >= n_second:
                     continue
                 for d_first in range(1, n_first):
-                    copy = pltpu.make_async_remote_copy(
-                        src_ref=piece(a, grads[a].at[0], spot(half, d_first, d_second), half),
-                        dst_ref=first_in[a].at[half, d_first - 1, d_second],
-                        send_sem=first_send.at[a, half, d_first - 1, d_second],
-                        recv_sem=first_recv.at[a, half, d_first - 1, d_second],
-                        device_id={"batch": spot(half, d_first, 0)},
+                    at = (half, d_first - 1, d_second)
+                    raw_loads[a, half, d_first, d_second].wait()
+                    encode(a, raw[a].at[at], first_out[a].at[at], first_unit[a].at[at])
+                    to = {"batch": spot(half, d_first, 0)}
+                    pair = (
+                        pltpu.make_async_remote_copy(
+                            src_ref=first_unit[a].at[at],
+                            dst_ref=first_unit_in[a].at[at],
+                            send_sem=first_unit_send.at[(a,) + at],
+                            recv_sem=first_unit_recv.at[(a,) + at],
+                            device_id=to,
+                        ),
+                        pltpu.make_async_remote_copy(
+                            src_ref=first_out[a].at[at],
+                            dst_ref=first_in[a].at[at],
+                            send_sem=first_send.at[(a,) + at],
+                            recv_sem=first_recv.at[(a,) + at],
+                            device_id=to,
+                        ),
                     )
-                    copy.start()
-                    first[a, half, d_first, d_second] = copy
+                    if entered:
+                        pair[0].start()
+                        pair[1].start()
+                    ready.append(pair)
+                    first[a, half, d_first, d_second] = pair
+            if not entered:
+                entered.append(True)
+                pl.semaphore_wait(barrier, n - 1 + m - 1)
+                for pair in ready:
+                    pair[0].start()
+                    pair[1].start()
 
     def send_small():
         for copy in small_loads:
@@ -146,19 +233,34 @@
                 loads[a, half, d_second].wait()
                 value = held[a][half, d_second]
                 for d_first in range(1, n_first):
-                    first[a, half, d_first, d_second].wait_recv()
-                    value = value + first_in[a][half, d_first - 1, d_second]
+                    for copy in first[a, half, d_first, d_second]:
+                        copy.wait_recv()
+                    at = (half, d_first - 1, d_second)
+                    value = value + decode(a, first_in[a].at[at], first_unit_in[a].at[at])
                 held[a][half, d_second] = value
                 if d_second > 0:
-                    copy = pltpu.make_async_remote_copy(
-                        src_ref=held[a].at[half, d_second],
-                        dst_ref=second_in[a].at[half, d_second - 1],
-                        send_sem=second_send.at[a, half, d_second - 1],
-                        recv_sem=second_recv.at[a, half, d_second - 1],
-                        device_id={"batch": spot(half, 0, d_second)},
+                    at = (half, d_second - 1)
+                    encode(a, held[a].at[half, d_second], second_out[a].at[at], second_unit[a].at[at])
+                    to = {"batch": spot(half, 0, d_second)}
+                    pair = (
+                        pltpu.make_async_remote_copy(
+                            src_ref=second_unit[a].at[at],
+                            dst_ref=second_unit_in[a].at[at],
+                            send_sem=second_unit_send.at[(a,) + at],
+                            recv_sem=second_unit_recv.at[(a,) + at],
+                            device_id=to,
+                        ),
+                        pltpu.make_async_remote_copy(
+                            src_ref=second_out[a].at[at],
+                            dst_ref=second_in[a].at[at],
+                            send_sem=second_send.at[(a,) + at],
+                            recv_sem=second_recv.at[(a,) + at],
+                            device_id=to,
+                        ),
                     )
-                    copy.start()
-                    second[a, half, d_second] = copy
+                    pair[0].start()
+                    pair[1].start()
+                    second[a, half, d_second] = pair
 
     exchange = {}
 
@@ -167,8 +269,10 @@
         for half in range(2):
             value = held[a][half, 0]
             for d_second in range(1, extents(half)[1]):
-                second[a, half, d_second].wait_recv()
-                value = value + second_in[a][half, d_second - 1]
+                for copy in second[a, half, d_second]:
+                    copy.wait_recv()
+                at = (half, d_second - 1)
+                value = value + decode(a, second_in[a].at[at], second_unit_in[a].at[at])
             total[a][half * depth : (half + 1) * depth] = value * rate
         squares[a, 1:2] = row_squares(a, total[a][...])
         own = pltpu.make_async_copy(squares.at[a], squares_in.at[a, col], square_own.at[a])
@@ -258,7 +362,11 @@
     )
     for step in ORDER:
         steps[step[0]](*map(int, step[1:]))
-    for copies_sent in (first, second, back, spread):
+    for pairs in (first, second):
+        for pair in pairs.values():
+            pair[0].wait_send()
+            pair[1].wait_send()
+    for copies_sent in (back, spread):
         for copy in copies_sent.values():
             copy.wait_send()
     for a in range(4):
@@ -303,6 +411,7 @@
         blocks = [w.shape for w in weights]
         slices = blocks[0][0]
         slabs = [(b[0] // 2, b[1]) for b in blocks]
+        lines = [(1, s[0]) for s in slabs[:3]] + [(1, slabs[3][1])]
         f32, bf16 = jnp.float32, jnp.bfloat16
         DMA = pltpu.SemaphoreType.DMA
         hops = max(most - 1, 1)
@@ -319,17 +428,27 @@
             in_specs=[hbm] * 12,
             out_specs=[vmem] * 10,
             scratch_shapes=(
-                [pltpu.VMEM((2, hops, most) + s, f32) for s in slabs]
-                + [pltpu.VMEM((2, hops) + s, f32) for s in slabs]
+                [pltpu.VMEM((2, hops, most) + s, bf16) for s in slabs]
+                + [pltpu.VMEM((2, hops) + s, bf16) for s in slabs]
                 + [pltpu.VMEM((2, most) + s, f32) for s in slabs]
                 + [pltpu.VMEM(b, f32) for b in blocks]
                 + [pltpu.VMEM(b, f32) for b in blocks]
+                + [pltpu.VMEM((2, hops, most) + s, f32) for s in slabs]
+                + [pltpu.VMEM((2, hops, most) + s, bf16) for s in slabs]
+                + [pltpu.VMEM((2, hops) + s, bf16) for s in slabs]
+                + [pltpu.VMEM((2, hops, most) + l, f32) for l in lines] * 2
+                + [pltpu.VMEM((2, hops) + l, f32) for l in lines] * 2
                 + [
                     pltpu.VMEM((4, 2, slices), f32),
                     pltpu.VMEM((4, m, 2, slices), f32),
                     pltpu.VMEM((n, 1, 2 * (n + 1) * width), f32),
                     DMA((4, 2, most)),
+                    DMA((4, 2, hops, most)),
                     DMA((4,)),
+                    DMA((4, 2, hops, most)),
+                    DMA((4, 2, hops, most)),
+                    DMA((4, 2, hops)),
+                    DMA((4, 2, hops)),
                     DMA((4, 2, hops, most)),
                     DMA((4, 2, hops, most)),
                     DMA((4, 2, hops)),

time: 115 us -> 82.2 us (0.71)
  Pallas kernels: 114 us -> 81.4 us
    pallas_call x1, Pallas kernels: 112 us -> 78.6 us  [per_device(): pl.pallas_call(functools.partial(kernel, n, m, n_x, n_y), out_shape=[pltp...]
where the time goes in v1:
time: 82.2 us; the launch traced here: 82.1 us
  Pallas kernels  81.4 us (99%)
    pallas_call x1, Pallas kernels, per_device(): pl.pallas_call(functools.partial(kernel, n, m, n_x, n_y), out_shape=[pltp...  78.6 us
    pallas_call x1, Pallas kernels, per_device(): pl.pallas_call(functools.partial(finish, n), out_shape=out_shape[:8] + [j...  2.78 us

profile of v1, /device:TPU:0, one launch (start us, length us, event | category | flops | bytes accessed | tf_op | source)
XLA Modules:
  0.0 82.1 jit_solution(5231724307524890434)
XLA Ops:
  0.6 78.6 %shard_map.211 = (bf16[2048,256]{1,0:T(8,128)(2,1)S(1)}, bf16[2048,256]{1,0:T(8,128)(2,1)S(1)}, bf16[2048,256]{1,0:T(8,128)(2,1)S(1)}, bf16[256,2048]{1,0:T(8,12...) custom-call(f32[1,2048,256]{2,1,0:T(8,128)} %refs_0_.1, ...), custom_call_target="tpu_custom_call" | custom-call | tf_op jit(solution)/shard_map/pallas_call | solution.py:425
  79.3 2.8 %shard_map.212 = (bf16[2048,256]{1,0:T(8,128)(2,1)}, bf16[2048,256]{1,0:T(8,128)(2,1)}, bf16[2048,256]{1,0:T(8,128)(2,1)}, bf16[256,2048]{1,0:T(8,128)(2,1)}, f3...) custom-call(bf16[2048,256]{1,0:T(8,128)(2,1)S(1)} %get-tuple-element, ...), custom_call_target="tpu_custom_call" | custom-call | tf_op jit(solution)/shard_map/pallas_call | solution.py:472

commit v2 on v0

v2 whole, which is shorter than its diff:
```python
import functools
import math

import jax
import jax.numpy as jnp
from jax import lax
from jax.experimental import pallas as pl
from jax.experimental.pallas import tpu as pltpu
from jax.sharding import PartitionSpec as P

learn_rate = 0.4
LANES = 128
LOW, SPAN, TINY = 87.0, 175.0, 1e-30
ORDER = (
    ("F0", "F1", "W0", "W1", "W2", "W3", "A0", "S", "F2", "A1", "F3", "E", "N", "B0")
    + ("A2", "B1", "U0", "A3", "B2", "U1", "P0", "M", "B3", "U2", "P1", "U3", "P2", "P3")
)


def across(a, line, depth):
    return jnp.broadcast_to(line, (LANES, depth)).T if a < 3 else line


def blocks_of(a, columns):
    step = LANES if a < 3 else columns
    return [slice(start, start + step) for start in range(0, columns, step)]


def encode(a, value, code, unit):
    depth, columns = value.shape
    size = jnp.abs(value)
    if a < 3:
        size = functools.reduce(jnp.maximum, [size[:, block] for block in blocks_of(a, columns)]).T
    largest = jnp.maximum(jnp.max(size, axis=0, keepdims=True), TINY)
    unit[...] = largest * SPAN**-2
    gain = across(a, SPAN**2 / largest, depth)
    for block in blocks_of(a, columns):
        part = value[:, block]
        level = jnp.abs(part) * gain
        level = jnp.exp(level * lax.rsqrt(level + TINY) - LOW)
        code[:, block] = jnp.where(part < 0, -level, level).astype(jnp.bfloat16)


def decode(a, code, unit):
    depth, columns = code.shape
    scale = across(a, unit[...], depth)
    parts = []
    for block in blocks_of(a, columns):
        part = code[:, block].astype(jnp.float32)
        root = jnp.log(jnp.abs(part)) + LOW
        level = root * root * scale
        parts.append(jnp.where(part < 0, -level, level))
    return jnp.concatenate(parts, axis=1) if len(parts) > 1 else parts[0]


def drain(ref, sem):
    pltpu.make_async_copy(ref, ref, sem).wait()


def kernel(n, m, n_x, n_y, *refs):
    grads, small_grads = refs[0:4], refs[4:6]
    weights, small_weights = refs[6:10], refs[10:12]
    copies, news = refs[12:16], refs[16:20]
    small_full, small_own = refs[20:22]
    scratch = refs[22:]
    full, total, own_weight = scratch[0:4], scratch[4:8], scratch[8:12]
    first_out, first_in = scratch[12:16], scratch[16:20]
    second_out, second_in = scratch[20:24], scratch[24:28]
    unit_out, first_unit, second_unit = scratch[28:32], scratch[32:36], scratch[36:40]
    squares, squares_in, small_hold, small_in, small_done = scratch[40:45]
    (
        early_sem, load_sem, weight_sem, small_local,
        send_sem, unit_send,
        first_recv, first_unit_recv, second_recv, second_unit_recv,
        square_send, square_recv, back_recv, spread_recv,
        small_sem, done_sem, plane_sem, row_sem,
    ) = scratch[45:]
    rate = n ** (-0.5)
    most = max(n_x, n_y)

    me = lax.axis_index("batch")
    col = lax.axis_index("cols")
    y, x = me // n_x, lax.rem(me, n_x)

    def spot(half, d_first, d_second):
        if half == 0:
            return lax.rem(y + d_second, n_y) * n_x + lax.rem(x + d_first, n_x)
        return lax.rem(y + d_first, n_y) * n_x + lax.rem(x + d_second, n_x)

    def extents(half):
        return (n_x, n_y) if half == 0 else (n_y, n_x)

    def piece(a, ref, chunk, half):
        rows, columns = total[a].shape
        depth = rows // 2
        if a < 3:
            start = pl.multiple_of(chunk * rows + half * depth, depth)
            return ref.at[pl.ds(start, depth), :]
        start = pl.multiple_of(chunk * columns, columns)
        return ref.at[pl.ds(half * depth, depth), pl.ds(start, columns)]

    def slots(a, ref, half):
        n_first, n_second = extents(half)
        return ref[a].at[half, pl.ds(0, n_first - 1), pl.ds(0, n_second)]

    odd = lax.rem(col, 2)
    pair = col - odd
    barrier = pltpu.get_barrier_semaphore()

    def greet(skip, **device):
        @pl.when(jnp.logical_not(skip))
        def _():
            pl.semaphore_signal(barrier, inc=1, device_id=device)

    neighbours = [spot(0, d, 0) for d in range(1, n_x)] + [spot(0, 0, d) for d in range(1, n_y)]
    for other in neighbours:
        pl.semaphore_signal(barrier, inc=1, device_id={"batch": other, "cols": pair})
    greet(odd == 0, batch=me, cols=pair)
    for d in range(0, m, 2):
        other = lax.rem(pair + d, m) + 1
        greet(other == col, batch=me, cols=other)

    def enter_plane():
        @pl.when(odd == 0)
        def _():
            pl.semaphore_wait(barrier, 2 * len(neighbours) + 1)
            pl.semaphore_signal(plane_sem, inc=1, device_id={"cols": col + 1})

        @pl.when(odd == 1)
        def _():
            pl.semaphore_wait(plane_sem, 1)

    def enter_row():
        @pl.when(odd == 1)
        def _():
            pl.semaphore_wait(barrier, m - 1)
            pl.semaphore_signal(row_sem, inc=1, device_id={"cols": col - 1})

        @pl.when(odd == 0)
        def _():
            pl.semaphore_wait(row_sem, 1)

    early, rest = {}, []
    for half in range(2):
        n_first, n_second = extents(half)
        for d_first in range(n_first):
            for d_second in range(n_second):
                here = spot(half, d_first, d_second)
                first_sent = d_first > 0 and d_second == n_second - 1
                copy = pltpu.make_async_copy(
                    piece(0, grads[0].at[0], here, half),
                    piece(0, full[0], here, half),
                    early_sem.at[half, d_first - 1] if first_sent else load_sem.at[0],
                )
                if first_sent:
                    early[half, d_first] = copy
                else:
                    rest.append(copy)
    width = small_weights[0].shape[1]
    shares, chunk = small_done.shape[0], small_done.shape[3]
    per_array = shares // 2
    share = lax.rem(col, shares)
    smalls, weight_loads = [], []
    for i in range(2):
        smalls.append((small_grads[i], small_hold.at[i, :, pl.ds(0, n * width)]))
        smalls.append((small_weights[i], small_hold.at[i, :, pl.ds(n * width, width)]))
    for copy in early.values():
        copy.start()
    for copy in rest:
        copy.start()
    for a in range(1, 4):
        pltpu.make_async_copy(grads[a].at[0], full[a], load_sem.at[a]).start()
        if a == 1:
            for b in range(4):
                weight_loads.append(pltpu.make_async_copy(weights[b], own_weight[b], weight_sem.at[b]))
                weight_loads[b].start()
            for source, target in smalls:
                pltpu.make_async_copy(source, target, small_local).start()

    def load_rest(a):
        if a == 0:
            drain(full[0].at[pl.ds(0, len(rest) * (total[0].shape[0] // 2))], load_sem.at[0])
        else:
            drain(full[a], load_sem.at[a])

    entered, loaded = [], set()

    def send(source, target, sem, arrival, device):
        pltpu.make_async_remote_copy(
            src_ref=source, dst_ref=target, send_sem=sem, recv_sem=arrival, device_id=device
        ).start()

    def send_first(a):
        for d in range(most - 1, -1, -1):
            for half in range(2):
                n_first, n_second = extents(half)
                for d_first in range(1, n_first):
                    if d >= n_second:
                        continue
                    if a == 0 and d == n_second - 1:
                        early[half, d_first].wait()
                    elif a not in loaded:
                        loaded.add(a)
                        load_rest(a)
                    at = (half, d_first - 1, d)
                    unit = unit_out[a].at[at]
                    encode(a, piece(a, full[a], spot(half, d_first, d), half)[...], first_out[a].at[at], unit)
                    if not entered:
                        entered.append(True)
                        enter_plane()
                    to = {"batch": spot(half, d_first, 0)}
                    send(unit, first_unit[a].at[at], unit_send.at[a], first_unit_recv.at[a], to)
                    send(first_out[a].at[at], first_in[a].at[at], send_sem.at[a], first_recv.at[a], to)

    def send_small():
        drain(small_hold, small_local)
        start = lax.rem(share, per_array) * chunk
        for k in range(n + 1):
            small_in[me, k] = small_hold[share // per_array, :, pl.ds(pl.multiple_of(k * width + start, chunk), chunk)]
        for d in range(1, n):
            send(small_in.at[me], small_in.at[me], small_sem.at[0], small_sem.at[1], {"batch": lax.rem(me + d, n)})

    def row_squares(a, value):
        value = value * value
        if a == 3:
            return jnp.sum(value, axis=0, keepdims=True)
        folded = value[:, :LANES]
        for start in range(LANES, value.shape[1], LANES):
            folded = folded + value[:, start : start + LANES]
        return jnp.sum(folded.T, axis=0, keepdims=True)

    def weigh(a):
        weight_loads[a].wait()
        squares[a, 0:1] = row_squares(a, own_weight[a][...])

    def drain_first(a, ref, sem):
        if n_x == n_y:
            drain(ref[a], sem)
        else:
            for half in range(2):
                if extents(half)[0] > 1:
                    drain(slots(a, ref, half), sem)

    def add_first(a):
        if a not in loaded:
            loaded.add(a)
            load_rest(a)
        drain_first(a, first_unit, first_unit_recv.at[a])
        drain_first(a, first_in, first_recv.at[a])
        for d_second in range(most - 1, -1, -1):
            for half in range(2):
                n_first, n_second = extents(half)
                if d_second >= n_second:
                    continue
                own = piece(a, full[a], spot(half, 0, d_second), half)
                value = own[...]
                for d_first in range(1, n_first):
                    at = (half, d_first - 1, d_second)
                    value = value + decode(a, first_in[a].at[at], first_unit[a].at[at])
                if d_second == 0:
                    own[...] = value
                    continue
                at = (half, d_second - 1)
                unit = unit_out[a].at[at + (most,)]
                encode(a, value, second_out[a].at[at], unit)
                to = {"batch": spot(half, 0, d_second)}
                send(unit, second_unit[a].at[at], unit_send.at[a], second_unit_recv.at[a], to)
                send(second_out[a].at[at], second_in[a].at[at], send_sem.at[a], second_recv.at[a], to)

    def used_second(a, ref):
        if n_x == n_y:
            return ref[a]
        half = 0 if n_y > 1 else 1
        return ref[a].at[half, pl.ds(0, extents(half)[1] - 1)]

    def add_second(a):
        drain(used_second(a, second_unit), second_unit_recv.at[a])
        drain(used_second(a, second_in), second_recv.at[a])
        depth = total[a].shape[0] // 2
        for half in range(2):
            value = piece(a, full[a], me, half)[...]
            for d_second in range(1, extents(half)[1]):
                at = (half, d_second - 1)
                value = value + decode(a, second_in[a].at[at], second_unit[a].at[at])
            total[a][half * depth : (half + 1) * depth] = value * rate
        squares[a, 1:2] = row_squares(a, total[a][...])
        squares_in[a, col] = squares[a]
        for d in range(1, m):
            send(squares.at[a], squares_in.at[a, col], square_send, square_recv.at[a], {"cols": lax.rem(col + d, m)})

    def send_spread(a, half, d_second):
        n_first, n_second = extents(half)
        slab = piece(a, copies[a], spot(half, 0, n_second - d_second), half)
        for d_first in range(1, n_first):
            send(slab, slab, send_sem.at[a], spread_recv.at[a], {"batch": spot(half, d_first, 0)})

    def update(a):
        drain(squares_in.at[a, pl.ds(0, m - 1)], square_recv.at[a])
        both = squares_in[a, 0]
        for d in range(1, m):
            both = both + squares_in[a, d]
        ratio = learn_rate * (jnp.sqrt(both[0:1]) * lax.rsqrt(both[1:2] + 1e-06))
        rows, columns = total[a].shape
        if a < 3:
            ratio = jnp.broadcast_to(ratio, (LANES, rows)).T
            for start in range(0, columns, LANES):
                block = slice(start, start + LANES)
                news[a][:, block] = own_weight[a][:, block] - total[a][:, block] * ratio
        else:
            news[a][...] = own_weight[a][...] - total[a][...] * ratio
        depth = rows // 2
        for half in range(2):
            piece(a, copies[a], me, half)[...] = news[a][half * depth : (half + 1) * depth].astype(jnp.bfloat16)
        for half in range(2):
            slab = piece(a, copies[a], me, half)
            for d_second in range(1, extents(half)[1]):
                send(slab, slab, send_sem.at[a], back_recv.at[a], {"batch": spot(half, 0, d_second)})
        for half in range(2):
            send_spread(a, half, 0)

    def pass_on(a):
        drain(used_second(a, second_in), back_recv.at[a])
        for half in range(2):
            for d_second in range(1, extents(half)[1]):
                send_spread(a, half, d_second)

    def update_small():
        drain(small_in.at[pl.ds(0, n - 1)], small_sem.at[1])
        for k in range(n):
            value = small_in[0, k]
            for j in range(1, n):
                value = value + small_in[j, k]
            small_done[share, k] = small_in[k, n] - learn_rate * (value * rate)
        for d in range(1, shares):
            to = {"cols": col - share + lax.rem(share + d, shares)}
            send(small_done.at[share], small_done.at[share], done_sem.at[0], done_sem.at[1], to)

    def gather_small():
        drain(small_done.at[pl.ds(0, shares - 1)], done_sem.at[1])
        for i in range(2):
            for k in range(n):
                for j in range(per_array):
                    small_full[i, k, :, j * chunk : (j + 1) * chunk] = small_done[i * per_array + j, k]
            small_own[i] = small_full[i, me]

    steps = dict(
        F=send_first, S=send_small, W=weigh, A=add_first, B=add_second, U=update, P=pass_on
    )
    steps.update(N=update_small, M=gather_small, E=enter_row)
    for step in ORDER:
        steps[step[0]](*map(int, step[1:]))
    drain(small_in.at[pl.ds(0, n - 1)], small_sem.at[0])
    drain(small_done.at[pl.ds(0, shares - 1)], done_sem.at[0])
    drain(squares_in.at[:, pl.ds(0, m - 1)], square_send)
    for a in range(4):
        drain(unit_out[a], unit_send.at[a])
    for a in range(4):
        rows, columns = full[a].shape
        slabs = 2 * sum((extents(h)[0] - 1) * extents(h)[1] + extents(h)[1] - 1 for h in range(2))
        sent = slabs * (total[a].shape[0] // 2) * total[a].shape[1] // 2
        drain(full[a].at[pl.ds(0, sent // columns)], send_sem.at[a])
        drain_first(a, first_in, spread_recv.at[a])


def finish(n, *refs):
    results, full, own = refs[0:8], refs[8], refs[9]
    outs, small_copies, small_news = refs[10:18], refs[18:20], refs[20:22]
    copy_rows, new_rows, sem, small_sem = refs[22:24], refs[24:26], refs[26], refs[27]
    moves = [pltpu.make_async_copy(results[i], outs[i], sem.at[i]) for i in range(8)]
    for move in moves:
        move.start()
    width = full.shape[-1]
    for i in range(2):
        for j in range(n):
            copy_rows[i][j * width : (j + 1) * width] = full[i, j, 0].astype(jnp.bfloat16)
        new_rows[i][...] = own[i, 0]
    for i in range(2):
        moves.append(pltpu.make_async_copy(copy_rows[i], small_copies[i], small_sem.at[i]))
        moves.append(pltpu.make_async_copy(new_rows[i], small_news[i], small_sem.at[2 + i]))
    for move in moves[8:]:
        move.start()
    for move in moves:
        move.wait()


def solution(mesh):
    n, m = mesh.shape["batch"], mesh.shape["cols"]
    n_x = math.isqrt(n)
    if n_x * n_x != n:
        n_x = n
    n_y = n // n_x
    most = max(n_x, n_y)

    def per_device(*args):
        args = args[:10] + tuple(w.reshape(1, -1) for w in args[10:])
        grads, weights, width = args[0:4], args[6:10], args[10].shape[1]
        blocks = [w.shape for w in weights]
        slices = blocks[0][0]
        slabs = [(b[0] // 2, b[1]) for b in blocks]
        lines = [(1, s[0]) for s in slabs[:3]] + [(1, slabs[3][1])]
        f32, bf16 = jnp.float32, jnp.bfloat16
        DMA = pltpu.SemaphoreType.DMA
        hops = max(most - 1, 1)
        pieces = math.gcd(max(width // LANES, 1), m // 2)
        hbm = pl.BlockSpec(memory_space=pltpu.HBM)
        vmem = pl.BlockSpec(memory_space=pltpu.VMEM)
        out_shape = (
            [jax.ShapeDtypeStruct(g.shape[1:], bf16) for g in grads]
            + [jax.ShapeDtypeStruct(b, f32) for b in blocks]
            + [jax.ShapeDtypeStruct((2, n, 1, width), f32), jax.ShapeDtypeStruct((2, 1, width), f32)]
        )
        results = pl.pallas_call(
            functools.partial(kernel, n, m, n_x, n_y),
            out_shape=[pltpu.VMEM(o.shape, o.dtype) for o in out_shape],
            in_specs=[hbm] * 12,
            out_specs=[vmem] * 10,
            scratch_shapes=(
                [pltpu.VMEM(g.shape[1:], f32) for g in grads]
                + [pltpu.VMEM(b, f32) for b in blocks] * 2
                + [pltpu.VMEM((2, hops, most) + s, bf16) for s in slabs] * 2
                + [pltpu.VMEM((2, hops) + s, bf16) for s in slabs] * 2
                + [pltpu.VMEM((2, hops, most + 1) + l, f32) for l in lines]
                + [pltpu.VMEM((2, hops, most) + l, f32) for l in lines]
                + [pltpu.VMEM((2, hops) + l, f32) for l in lines]
                + [
                    pltpu.VMEM((4, 2, slices), f32),
                    pltpu.VMEM((4, m, 2, slices), f32),
                    pltpu.VMEM((2, 1, (n + 1) * width), f32),
                    pltpu.VMEM((n, n + 1, 1, width // pieces), f32),
                    pltpu.VMEM((2 * pieces, n, 1, width // pieces), f32),
                    DMA((2, hops)),
                    DMA((4,)),
                    DMA((4,)),
                    DMA,
                ]
                + [DMA((4,))] * 6
                + [DMA, DMA((4,)), DMA((4,)), DMA((4,)), DMA((2,)), DMA((2,))]
                + [pltpu.SemaphoreType.REGULAR] * 2
            ),
            compiler_params=pltpu.CompilerParams(
                collective_id=0, has_side_effects=True, vmem_limit_bytes=40 * 2**20
            ),
        )(*[pltpu.with_memory_space_constraint(v, pltpu.HBM) for v in args])
        done = pl.pallas_call(
            functools.partial(finish, n),
            out_shape=out_shape[:8]
            + [jax.ShapeDtypeStruct((n * width,), bf16)] * 2
            + [jax.ShapeDtypeStruct((width,), f32)] * 2,
            in_specs=[vmem] * 10,
            out_specs=[hbm] * 12,
            scratch_shapes=[pltpu.VMEM((n * width,), bf16)] * 2
            + [pltpu.VMEM((width,), f32)] * 2
            + [DMA((8,)), DMA((4,))],
            compiler_params=pltpu.CompilerParams(vmem_limit_bytes=2**20),
        )(*results)
        return tuple(done[0:4]) + tuple(done[8:10]) + tuple(done[4:8]) + tuple(done[10:12])

    in_specs = (
        (P("batch", None, "cols"),) * 3
        + (P("batch", "cols", None),)
        + (P("batch", None),) * 2
        + (P("batch", "cols"),) * 3
        + (P("cols", "batch"),)
        + (P("batch"),) * 2
    )
    out_specs = (
        (P(None, "cols"),) * 3
        + (P("cols", None),)
        + (P(),) * 2
        + (P("batch", "cols"),) * 3
        + (P("cols", "batch"),)
        + (P("batch"),) * 2
    )
    return jax.shard_map(per_device, mesh=mesh, in_specs=in_specs, out_specs=out_specs, check_vma=False)
```

time: 115 us -> 78.1 us (0.68)
  Pallas kernels: 114 us -> 77.3 us
    pallas_call x1, Pallas kernels: 112 us -> 74.5 us  [per_device(): pl.pallas_call(functools.partial(kernel, n, m, n_x, n_y), out_shape=[pltp...]
where the time goes in v2:
time: 78.1 us; the launch traced here: 78 us
  Pallas kernels  77.3 us (99%)
    pallas_call x1, Pallas kernels, per_device(): pl.pallas_call(functools.partial(kernel, n, m, n_x, n_y), out_shape=[pltp...  74.5 us
    pallas_call x1, Pallas kernels, per_device(): pl.pallas_call(functools.partial(finish, n), out_shape=out_shape[:8] + [j...  2.78 us

profile of v2, /device:TPU:0, one launch (start us, length us, event | category | flops | bytes accessed | tf_op | source)
XLA Modules:
  0.0 78.0 jit_solution(6963079225660582569)
XLA Ops:
  0.6 74.5 %shard_map.211 = (bf16[2048,256]{1,0:T(8,128)(2,1)S(1)}, bf16[2048,256]{1,0:T(8,128)(2,1)S(1)}, bf16[2048,256]{1,0:T(8,128)(2,1)S(1)}, bf16[256,2048]{1,0:T(8,12...) custom-call(f32[1,2048,256]{2,1,0:T(8,128)} %refs_0_.1, ...), custom_call_target="tpu_custom_call" | custom-call | tf_op jit(solution)/shard_map/pallas_call | solution.py:412
  75.2 2.8 %shard_map.212 = (bf16[2048,256]{1,0:T(8,128)(2,1)}, bf16[2048,256]{1,0:T(8,128)(2,1)}, bf16[2048,256]{1,0:T(8,128)(2,1)}, bf16[256,2048]{1,0:T(8,128)(2,1)}, f3...) custom-call(bf16[2048,256]{1,0:T(8,128)(2,1)S(1)} %get-tuple-element, ...), custom_call_target="tpu_custom_call" | custom-call | tf_op jit(solution)/shard_map/pallas_call | solution.py:444

commit v3 on v2

--- a/solution.py
+++ b/solution.py
@@ -11,9 +11,9 @@
 learn_rate = 0.4
 LANES = 128
 LOW, SPAN, TINY = 87.0, 175.0, 1e-30
+TURNED = 2
 ORDER = (
-    ("F0", "F1", "W0", "W1", "W2", "W3", "A0", "S", "F2", "A1", "F3", "E", "N", "B0")
-    + ("A2", "B1", "U0", "A3", "B2", "U1", "P0", "M", "B3", "U2", "P1", "U3", "P2", "P3")
+    ('F0', 'F1', 'W0', 'W1', 'W2', 'W3', 'A0', 'S', 'F2', 'A1', 'F3', 'G2', 'E', 'N', 'B0', 'B1', 'U0', 'A2', 'A3', 'B2', 'U1', 'P0', 'M', 'B3', 'U2', 'P1', 'U3', 'P2', 'P3')
 )
 
 
@@ -42,8 +42,8 @@
 
 
 def decode(a, code, unit):
-    depth, columns = code.shape
-    scale = across(a, unit[...], depth)
+    rows, columns = code.shape
+    scale = across(a, unit[...], unit.shape[1])[:rows]
     parts = []
     for block in blocks_of(a, columns):
         part = code[:, block].astype(jnp.float32)
@@ -57,7 +57,7 @@
     pltpu.make_async_copy(ref, ref, sem).wait()
 
 
-def kernel(n, m, n_x, n_y, *refs):
+def kernel(n, m, n_x, n_y, turned, *refs):
     grads, small_grads = refs[0:4], refs[4:6]
     weights, small_weights = refs[6:10], refs[10:12]
     copies, news = refs[12:16], refs[16:20]
@@ -68,13 +68,14 @@
     second_out, second_in = scratch[20:24], scratch[24:28]
     unit_out, first_unit, second_unit = scratch[28:32], scratch[32:36], scratch[36:40]
     squares, squares_in, small_hold, small_in, small_done = scratch[40:45]
+    turned_in, turned_unit = scratch[45:47]
     (
         early_sem, load_sem, weight_sem, small_local,
         send_sem, unit_send,
         first_recv, first_unit_recv, second_recv, second_unit_recv,
         square_send, square_recv, back_recv, spread_recv,
-        small_sem, done_sem, plane_sem, row_sem,
-    ) = scratch[45:]
+        small_sem, done_sem, turned_sem, plane_sem, row_sem,
+    ) = scratch[47:]
     rate = n ** (-0.5)
     most = max(n_x, n_y)
 
@@ -104,7 +105,8 @@
         return ref[a].at[half, pl.ds(0, n_first - 1), pl.ds(0, n_second)]
 
     odd = lax.rem(col, 2)
-    pair = col - odd
+    row_col = col - odd
+    plane_col = row_col + 1
     barrier = pltpu.get_barrier_semaphore()
 
     def greet(skip, **device):
@@ -114,29 +116,29 @@
 
     neighbours = [spot(0, d, 0) for d in range(1, n_x)] + [spot(0, 0, d) for d in range(1, n_y)]
     for other in neighbours:
-        pl.semaphore_signal(barrier, inc=1, device_id={"batch": other, "cols": pair})
-    greet(odd == 0, batch=me, cols=pair)
+        pl.semaphore_signal(barrier, inc=1, device_id={"batch": other, "cols": plane_col})
+    greet(odd == 1, batch=me, cols=plane_col)
     for d in range(0, m, 2):
-        other = lax.rem(pair + d, m) + 1
+        other = lax.rem(row_col + d, m)
         greet(other == col, batch=me, cols=other)
 
     def enter_plane():
+        @pl.when(odd == 1)
+        def _():
+            pl.semaphore_wait(barrier, 2 * len(neighbours) + 1)
+            pl.semaphore_signal(plane_sem, inc=1, device_id={"cols": row_col})
+
         @pl.when(odd == 0)
         def _():
-            pl.semaphore_wait(barrier, 2 * len(neighbours) + 1)
-            pl.semaphore_signal(plane_sem, inc=1, device_id={"cols": col + 1})
+            pl.semaphore_wait(plane_sem, 1)
+
+    def enter_row():
+        @pl.when(odd == 0)
+        def _():
+            pl.semaphore_wait(barrier, m - 1)
+            pl.semaphore_signal(row_sem, inc=1, device_id={"cols": plane_col})
 
         @pl.when(odd == 1)
-        def _():
-            pl.semaphore_wait(plane_sem, 1)
-
-    def enter_row():
-        @pl.when(odd == 1)
-        def _():
-            pl.semaphore_wait(barrier, m - 1)
-            pl.semaphore_signal(row_sem, inc=1, device_id={"cols": col - 1})
-
-        @pl.when(odd == 0)
         def _():
             pl.semaphore_wait(row_sem, 1)
 
@@ -183,15 +185,50 @@
         else:
             drain(full[a], load_sem.at[a])
 
-    entered, loaded = [], set()
+    entered, loaded, ready = [], set(), []
 
     def send(source, target, sem, arrival, device):
         pltpu.make_async_remote_copy(
             src_ref=source, dst_ref=target, send_sem=sem, recv_sem=arrival, device_id=device
         ).start()
 
-    def send_first(a):
-        for d in range(most - 1, -1, -1):
+    def send_turned(half):
+        a, at, top = TURNED, (half, 0, 1), pl.ds(0, turned)
+        turns = me == (1 if half == 0 else 2)
+        std = {"batch": spot(half, 1, 0)}
+        code = first_out[a].at[at + (top,)]
+        below = pl.ds(turned, total[a].shape[0] // 2 - turned)
+        send(first_out[a].at[at + (below,)], first_in[a].at[at + (below,)], send_sem.at[a], first_recv.at[a], std)
+
+        @pl.when(jnp.logical_not(turns))
+        def _():
+            send(code, first_in[a].at[at + (top,)], send_sem.at[a], first_recv.at[a], std)
+
+        @pl.when(turns)
+        def _():
+            far = {"batch": n - 1}
+            send(unit_out[a].at[at], turned_unit.at[half], turned_sem.at[0], turned_sem.at[1], far)
+            send(code, turned_in.at[half], send_sem.at[a], turned_sem.at[2], far)
+
+    def add_turned(a):
+        if a not in loaded:
+            loaded.add(a)
+            load_rest(a)
+        if turned and a == TURNED:
+            @pl.when(me == n - 1)
+            def _():
+                drain(turned_unit, turned_sem.at[1])
+                drain(turned_in, turned_sem.at[2])
+                for half in range(2):
+                    own = piece(a, full[a], spot(half, 1, 0), half).at[pl.ds(0, turned)]
+                    own[...] = own[...] + decode(a, turned_in.at[half], turned_unit.at[half])
+
+        send_first(a, [0])
+
+    def send_first(a, ds=None):
+        if ds is None:
+            ds = range(most - 1, -1 if a != TURNED else 0, -1)
+        for d in ds:
             for half in range(2):
                 n_first, n_second = extents(half)
                 for d_first in range(1, n_first):
@@ -205,12 +242,18 @@
                     at = (half, d_first - 1, d)
                     unit = unit_out[a].at[at]
                     encode(a, piece(a, full[a], spot(half, d_first, d), half)[...], first_out[a].at[at], unit)
-                    if not entered:
-                        entered.append(True)
-                        enter_plane()
                     to = {"batch": spot(half, d_first, 0)}
-                    send(unit, first_unit[a].at[at], unit_send.at[a], first_unit_recv.at[a], to)
-                    send(first_out[a].at[at], first_in[a].at[at], send_sem.at[a], first_recv.at[a], to)
+                    ready.append((unit, first_unit[a].at[at], unit_send.at[a], first_unit_recv.at[a], to))
+                    if turned and a == TURNED and d == 1:
+                        ready.append((half,))
+                    else:
+                        ready.append((first_out[a].at[at], first_in[a].at[at], send_sem.at[a], first_recv.at[a], to))
+            if not entered:
+                entered.append(True)
+                enter_plane()
+            for item in ready:
+                send_turned(*item) if len(item) == 1 else send(*item)
+            ready.clear()
 
     def send_small():
         drain(small_hold, small_local)
@@ -246,7 +289,16 @@
             loaded.add(a)
             load_rest(a)
         drain_first(a, first_unit, first_unit_recv.at[a])
-        drain_first(a, first_in, first_recv.at[a])
+        if turned and a == TURNED:
+            @pl.when(me == 0)
+            def _():
+                drain(full[a].at[pl.ds(0, total[a].shape[0] - turned)], first_recv.at[a])
+
+            @pl.when(me != 0)
+            def _():
+                drain_first(a, first_in, first_recv.at[a])
+        else:
+            drain_first(a, first_in, first_recv.at[a])
         for d_second in range(most - 1, -1, -1):
             for half in range(2):
                 n_first, n_second = extents(half)
@@ -256,7 +308,10 @@
                 value = own[...]
                 for d_first in range(1, n_first):
                     at = (half, d_first - 1, d_second)
-                    value = value + decode(a, first_in[a].at[at], first_unit[a].at[at])
+                    before, value = value, value + decode(a, first_in[a].at[at], first_unit[a].at[at])
+                    if turned and a == TURNED and d_second == 1:
+                        top = jnp.where(me == 0, before[:turned], value[:turned])
+                        value = jnp.concatenate([top, value[turned:]], axis=0)
                 if d_second == 0:
                     own[...] = value
                     continue
@@ -344,7 +399,7 @@
             small_own[i] = small_full[i, me]
 
     steps = dict(
-        F=send_first, S=send_small, W=weigh, A=add_first, B=add_second, U=update, P=pass_on
+        F=send_first, G=add_turned, S=send_small, W=weigh, A=add_first, B=add_second, U=update, P=pass_on
     )
     steps.update(N=update_small, M=gather_small, E=enter_row)
     for step in ORDER:
@@ -354,6 +409,10 @@
     drain(squares_in.at[:, pl.ds(0, m - 1)], square_send)
     for a in range(4):
         drain(unit_out[a], unit_send.at[a])
+    if turned:
+        @pl.when(jnp.logical_or(me == 1, me == 2))
+        def _():
+            drain(turned_unit.at[0], turned_sem.at[0])
     for a in range(4):
         rows, columns = full[a].shape
         slabs = 2 * sum((extents(h)[0] - 1) * extents(h)[1] + extents(h)[1] - 1 for h in range(2))
@@ -401,6 +460,7 @@
         f32, bf16 = jnp.float32, jnp.bfloat16
         DMA = pltpu.SemaphoreType.DMA
         hops = max(most - 1, 1)
+        turned = slabs[TURNED][0] * 6 // 256 * 16 if n_x == n_y == 2 else 0
         pieces = math.gcd(max(width // LANES, 1), m // 2)
         hbm = pl.BlockSpec(memory_space=pltpu.HBM)
         vmem = pl.BlockSpec(memory_space=pltpu.VMEM)
@@ -410,7 +470,7 @@
             + [jax.ShapeDtypeStruct((2, n, 1, width), f32), jax.ShapeDtypeStruct((2, 1, width), f32)]
         )
         results = pl.pallas_call(
-            functools.partial(kernel, n, m, n_x, n_y),
+            functools.partial(kernel, n, m, n_x, n_y, turned),
             out_shape=[pltpu.VMEM(o.shape, o.dtype) for o in out_shape],
             in_specs=[hbm] * 12,
             out_specs=[vmem] * 10,
@@ -428,13 +488,15 @@
                     pltpu.VMEM((2, 1, (n + 1) * width), f32),
                     pltpu.VMEM((n, n + 1, 1, width // pieces), f32),
                     pltpu.VMEM((2 * pieces, n, 1, width // pieces), f32),
+                    pltpu.VMEM((2, max(turned, 16)) + slabs[TURNED][1:], bf16),
+                    pltpu.VMEM((2,) + lines[TURNED], f32),
                     DMA((2, hops)),
                     DMA((4,)),
                     DMA((4,)),
                     DMA,
                 ]
                 + [DMA((4,))] * 6
-                + [DMA, DMA((4,)), DMA((4,)), DMA((4,)), DMA((2,)), DMA((2,))]
+                + [DMA, DMA((4,)), DMA((4,)), DMA((4,)), DMA((2,)), DMA((2,)), DMA((3,))]
                 + [pltpu.SemaphoreType.REGULAR] * 2
             ),
             compiler_params=pltpu.CompilerParams(

time: 78.1 us -> 76.6 us (0.981)
  Pallas kernels: 77.3 us -> 75.8 us
    pallas_call x1, Pallas kernels: 74.5 us -> 73 us  [per_device(): pl.pallas_call(functools.partial(kernel, n, m, n_x, n_y, turned), out_sha...]
where the time goes in v3:
time: 76.6 us; the launch traced here: 76.4 us
  Pallas kernels  75.8 us (99%)
    pallas_call x1, Pallas kernels, per_device(): pl.pallas_call(functools.partial(kernel, n, m, n_x, n_y, turned), out_sha...  73 us
    pallas_call x1, Pallas kernels, per_device(): pl.pallas_call(functools.partial(finish, n), out_shape=out_shape[:8] + [j...  2.78 us

profile of v3, /device:TPU:0, one launch (start us, length us, event | category | flops | bytes accessed | tf_op | source)
XLA Modules:
  0.0 76.4 jit_solution(6898442802716938950)
XLA Ops:
  0.6 73.0 %shard_map.211 = (bf16[2048,256]{1,0:T(8,128)(2,1)S(1)}, bf16[2048,256]{1,0:T(8,128)(2,1)S(1)}, bf16[2048,256]{1,0:T(8,128)(2,1)S(1)}, bf16[256,2048]{1,0:T(8,12...) custom-call(f32[1,2048,256]{2,1,0:T(8,128)} %refs_0_.1, ...), custom_call_target="tpu_custom_call" | custom-call | tf_op jit(solution)/shard_map/pallas_call | solution.py:472
  73.6 2.8 %shard_map.212 = (bf16[2048,256]{1,0:T(8,128)(2,1)}, bf16[2048,256]{1,0:T(8,128)(2,1)}, bf16[2048,256]{1,0:T(8,128)(2,1)}, bf16[256,2048]{1,0:T(8,128)(2,1)}, f3...) custom-call(bf16[2048,256]{1,0:T(8,128)(2,1)S(1)} %get-tuple-element, ...), custom_call_target="tpu_custom_call" | custom-call | tf_op jit(solution)/shard_map/pallas_call | solution.py:506

commit v4 on v3

--- a/solution.py
+++ b/solution.py
@@ -13,7 +13,7 @@
 LOW, SPAN, TINY = 87.0, 175.0, 1e-30
 TURNED = 2
 ORDER = (
-    ('F0', 'F1', 'W0', 'W1', 'W2', 'W3', 'A0', 'S', 'F2', 'A1', 'F3', 'G2', 'E', 'N', 'B0', 'B1', 'U0', 'A2', 'A3', 'B2', 'U1', 'P0', 'M', 'B3', 'U2', 'P1', 'U3', 'P2', 'P3')
+    ('F0', 'F1', 'F2', 'W0', 'W1', 'W2', 'W3', 'A0', 'S', 'A1', 'G2', 'F3', 'E', 'N', 'B0', 'B1', 'A2', 'U0', 'A3', 'U1', 'B2', 'B3', 'P0', 'M', 'U2', 'U3', 'P1', 'P2', 'P3')
 )
 
 
@@ -71,11 +71,13 @@
     turned_in, turned_unit = scratch[45:47]
     (
         early_sem, load_sem, weight_sem, small_local,
-        send_sem, unit_send,
+        unit_send,
         first_recv, first_unit_recv, second_recv, second_unit_recv,
-        square_send, square_recv, back_recv, spread_recv,
-        small_sem, done_sem, turned_sem, plane_sem, row_sem,
+        square_send, square_recv,
+        small_arrived, done_sem, turned_sem, plane_sem, row_sem,
     ) = scratch[47:]
+    sent = (early_sem,) + tuple(load_sem.at[a] for a in range(1, 4))
+    back_recv, spread_recv = first_unit_recv, first_recv
     rate = n ** (-0.5)
     most = max(n_x, n_y)
 
@@ -152,7 +154,7 @@
                 copy = pltpu.make_async_copy(
                     piece(0, grads[0].at[0], here, half),
                     piece(0, full[0], here, half),
-                    early_sem.at[half, d_first - 1] if first_sent else load_sem.at[0],
+                    early_sem if first_sent else load_sem.at[0],
                 )
                 if first_sent:
                     early[half, d_first] = copy
@@ -198,17 +200,17 @@
         std = {"batch": spot(half, 1, 0)}
         code = first_out[a].at[at + (top,)]
         below = pl.ds(turned, total[a].shape[0] // 2 - turned)
-        send(first_out[a].at[at + (below,)], first_in[a].at[at + (below,)], send_sem.at[a], first_recv.at[a], std)
+        send(first_out[a].at[at + (below,)], first_in[a].at[at + (below,)], sent[a], first_recv.at[a], std)
 
         @pl.when(jnp.logical_not(turns))
         def _():
-            send(code, first_in[a].at[at + (top,)], send_sem.at[a], first_recv.at[a], std)
+            send(code, first_in[a].at[at + (top,)], sent[a], first_recv.at[a], std)
 
         @pl.when(turns)
         def _():
             far = {"batch": n - 1}
             send(unit_out[a].at[at], turned_unit.at[half], turned_sem.at[0], turned_sem.at[1], far)
-            send(code, turned_in.at[half], send_sem.at[a], turned_sem.at[2], far)
+            send(code, turned_in.at[half], sent[a], turned_sem.at[2], far)
 
     def add_turned(a):
         if a not in loaded:
@@ -235,7 +237,9 @@
                     if d >= n_second:
                         continue
                     if a == 0 and d == n_second - 1:
-                        early[half, d_first].wait()
+                        if early:
+                            drain(full[0].at[pl.ds(0, len(early) * (total[0].shape[0] // 2))], early_sem)
+                            early.clear()
                     elif a not in loaded:
                         loaded.add(a)
                         load_rest(a)
@@ -247,7 +251,7 @@
                     if turned and a == TURNED and d == 1:
                         ready.append((half,))
                     else:
-                        ready.append((first_out[a].at[at], first_in[a].at[at], send_sem.at[a], first_recv.at[a], to))
+                        ready.append((first_out[a].at[at], first_in[a].at[at], sent[a], first_recv.at[a], to))
             if not entered:
                 entered.append(True)
                 enter_plane()
@@ -261,7 +265,7 @@
         for k in range(n + 1):
             small_in[me, k] = small_hold[share // per_array, :, pl.ds(pl.multiple_of(k * width + start, chunk), chunk)]
         for d in range(1, n):
-            send(small_in.at[me], small_in.at[me], small_sem.at[0], small_sem.at[1], {"batch": lax.rem(me + d, n)})
+            send(small_in.at[me], small_in.at[me], small_local, small_arrived, {"batch": lax.rem(me + d, n)})
 
     def row_squares(a, value):
         value = value * value
@@ -320,7 +324,7 @@
                 encode(a, value, second_out[a].at[at], unit)
                 to = {"batch": spot(half, 0, d_second)}
                 send(unit, second_unit[a].at[at], unit_send.at[a], second_unit_recv.at[a], to)
-                send(second_out[a].at[at], second_in[a].at[at], send_sem.at[a], second_recv.at[a], to)
+                send(second_out[a].at[at], second_in[a].at[at], sent[a], second_recv.at[a], to)
 
     def used_second(a, ref):
         if n_x == n_y:
@@ -347,7 +351,7 @@
         n_first, n_second = extents(half)
         slab = piece(a, copies[a], spot(half, 0, n_second - d_second), half)
         for d_first in range(1, n_first):
-            send(slab, slab, send_sem.at[a], spread_recv.at[a], {"batch": spot(half, d_first, 0)})
+            send(slab, slab, sent[a], spread_recv.at[a], {"batch": spot(half, d_first, 0)})
 
     def update(a):
         drain(squares_in.at[a, pl.ds(0, m - 1)], square_recv.at[a])
@@ -369,7 +373,7 @@
         for half in range(2):
             slab = piece(a, copies[a], me, half)
             for d_second in range(1, extents(half)[1]):
-                send(slab, slab, send_sem.at[a], back_recv.at[a], {"batch": spot(half, 0, d_second)})
+                send(slab, slab, sent[a], back_recv.at[a], {"batch": spot(half, 0, d_second)})
         for half in range(2):
             send_spread(a, half, 0)
 
@@ -380,7 +384,7 @@
                 send_spread(a, half, d_second)
 
     def update_small():
-        drain(small_in.at[pl.ds(0, n - 1)], small_sem.at[1])
+        drain(small_in.at[pl.ds(0, n - 1)], small_arrived)
         for k in range(n):
             value = small_in[0, k]
             for j in range(1, n):
@@ -404,7 +408,7 @@
     steps.update(N=update_small, M=gather_small, E=enter_row)
     for step in ORDER:
         steps[step[0]](*map(int, step[1:]))
-    drain(small_in.at[pl.ds(0, n - 1)], small_sem.at[0])
+    drain(small_in.at[pl.ds(0, n - 1)], small_local)
     drain(small_done.at[pl.ds(0, shares - 1)], done_sem.at[0])
     drain(squares_in.at[:, pl.ds(0, m - 1)], square_send)
     for a in range(4):
@@ -416,8 +420,8 @@
     for a in range(4):
         rows, columns = full[a].shape
         slabs = 2 * sum((extents(h)[0] - 1) * extents(h)[1] + extents(h)[1] - 1 for h in range(2))
-        sent = slabs * (total[a].shape[0] // 2) * total[a].shape[1] // 2
-        drain(full[a].at[pl.ds(0, sent // columns)], send_sem.at[a])
+        gone = slabs * (total[a].shape[0] // 2) * total[a].shape[1] // 2
+        drain(full[a].at[pl.ds(0, gone // columns)], sent[a])
         drain_first(a, first_in, spread_recv.at[a])
 
 
@@ -490,13 +494,13 @@
                     pltpu.VMEM((2 * pieces, n, 1, width // pieces), f32),
                     pltpu.VMEM((2, max(turned, 16)) + slabs[TURNED][1:], bf16),
                     pltpu.VMEM((2,) + lines[TURNED], f32),
-                    DMA((2, hops)),
+                    DMA,
                     DMA((4,)),
                     DMA((4,)),
                     DMA,
                 ]
-                + [DMA((4,))] * 6
-                + [DMA, DMA((4,)), DMA((4,)), DMA((4,)), DMA((2,)), DMA((2,)), DMA((3,))]
+                + [DMA((4,))] * 5
+                + [DMA, DMA((4,)), DMA, DMA((2,)), DMA((3,))]
                 + [pltpu.SemaphoreType.REGULAR] * 2
             ),
             compiler_params=pltpu.CompilerParams(

time: 76.6 us -> 76.3 us (level)
  no operation moved by 1% of the time
where the time goes in v4:
time: 76.3 us; the launch traced here: 76.1 us
  Pallas kernels  75.5 us (99%)
    pallas_call x1, Pallas kernels, per_device(): pl.pallas_call(functools.partial(kernel, n, m, n_x, n_y, turned), out_sha...  72.7 us
    pallas_call x1, Pallas kernels, per_device(): pl.pallas_call(functools.partial(finish, n), out_shape=out_shape[:8] + [j...  2.78 us

profile of v4, /device:TPU:0, one launch (start us, length us, event | category | flops | bytes accessed | tf_op | source)
XLA Modules:
  0.0 76.1 jit_solution(14580169262509173827)
XLA Ops:
  0.6 72.7 %shard_map.211 = (bf16[2048,256]{1,0:T(8,128)(2,1)S(1)}, bf16[2048,256]{1,0:T(8,128)(2,1)S(1)}, bf16[2048,256]{1,0:T(8,128)(2,1)S(1)}, bf16[256,2048]{1,0:T(8,12...) custom-call(f32[1,2048,256]{2,1,0:T(8,128)} %refs_0_.1, ...), custom_call_target="tpu_custom_call" | custom-call | tf_op jit(solution)/shard_map/pallas_call | solution.py:476
  73.4 2.8 %shard_map.212 = (bf16[2048,256]{1,0:T(8,128)(2,1)}, bf16[2048,256]{1,0:T(8,128)(2,1)}, bf16[2048,256]{1,0:T(8,128)(2,1)}, bf16[256,2048]{1,0:T(8,128)(2,1)}, f3...) custom-call(bf16[2048,256]{1,0:T(8,128)(2,1)S(1)} %get-tuple-element, ...), custom_call_target="tpu_custom_call" | custom-call | tf_op jit(solution)/shard_map/pallas_call | solution.py:510

commit v5 on v4

--- a/solution.py
+++ b/solution.py
@@ -13,7 +13,8 @@
 LOW, SPAN, TINY = 87.0, 175.0, 1e-30
 TURNED = 2
 ORDER = (
-    ('F0', 'F1', 'F2', 'W0', 'W1', 'W2', 'W3', 'A0', 'S', 'A1', 'G2', 'F3', 'E', 'N', 'B0', 'B1', 'A2', 'U0', 'A3', 'U1', 'B2', 'B3', 'P0', 'M', 'U2', 'U3', 'P1', 'P2', 'P3')
+    ("F0", "W0", "W1", "W2", "W3", "F1", "F2", "A0", "S", "A1", "G2", "F3", "E", "N", "B0", "B1")
+    + ("A2", "U0", "A3", "U1", "B2", "B3", "P0", "M", "U2", "U3", "P1", "P2", "P3")
 )
 
 
@@ -60,9 +61,10 @@
 def kernel(n, m, n_x, n_y, turned, *refs):
     grads, small_grads = refs[0:4], refs[4:6]
     weights, small_weights = refs[6:10], refs[10:12]
-    copies, news = refs[12:16], refs[16:20]
-    small_full, small_own = refs[20:22]
-    scratch = refs[22:]
+    copies = [refs[12].at[a] for a in range(3)] + [refs[13]]
+    news = [refs[14].at[a] for a in range(3)] + [refs[15]]
+    small_full, small_own = refs[16:18]
+    scratch = refs[18:]
     full, total, own_weight = scratch[0:4], scratch[4:8], scratch[8:12]
     first_out, first_in = scratch[12:16], scratch[16:20]
     second_out, second_in = scratch[20:24], scratch[24:28]
@@ -71,13 +73,15 @@
     turned_in, turned_unit = scratch[45:47]
     (
         early_sem, load_sem, weight_sem, small_local,
-        unit_send,
-        first_recv, first_unit_recv, second_recv, second_unit_recv,
+        unit_first,
+        first_recv, first_unit_recv, second_later, second_unit_recv,
         square_send, square_recv,
         small_arrived, done_sem, turned_sem, plane_sem, row_sem,
     ) = scratch[47:]
     sent = (early_sem,) + tuple(load_sem.at[a] for a in range(1, 4))
     back_recv, spread_recv = first_unit_recv, first_recv
+    unit_sent = (unit_first,) + tuple(weight_sem.at[a] for a in range(1, 4))
+    second_recv = (load_sem.at[0],) + tuple(second_later.at[a - 1] for a in range(1, 4))
     rate = n ** (-0.5)
     most = max(n_x, n_y)
 
@@ -247,7 +251,7 @@
                     unit = unit_out[a].at[at]
                     encode(a, piece(a, full[a], spot(half, d_first, d), half)[...], first_out[a].at[at], unit)
                     to = {"batch": spot(half, d_first, 0)}
-                    ready.append((unit, first_unit[a].at[at], unit_send.at[a], first_unit_recv.at[a], to))
+                    ready.append((unit, first_unit[a].at[at], unit_sent[a], first_unit_recv.at[a], to))
                     if turned and a == TURNED and d == 1:
                         ready.append((half,))
                     else:
@@ -323,8 +327,8 @@
                 unit = unit_out[a].at[at + (most,)]
                 encode(a, value, second_out[a].at[at], unit)
                 to = {"batch": spot(half, 0, d_second)}
-                send(unit, second_unit[a].at[at], unit_send.at[a], second_unit_recv.at[a], to)
-                send(second_out[a].at[at], second_in[a].at[at], sent[a], second_recv.at[a], to)
+                send(unit, second_unit[a].at[at], unit_sent[a], second_unit_recv.at[a], to)
+                send(second_out[a].at[at], second_in[a].at[at], sent[a], second_recv[a], to)
 
     def used_second(a, ref):
         if n_x == n_y:
@@ -334,7 +338,7 @@
 
     def add_second(a):
         drain(used_second(a, second_unit), second_unit_recv.at[a])
-        drain(used_second(a, second_in), second_recv.at[a])
+        drain(used_second(a, second_in), second_recv[a])
         depth = total[a].shape[0] // 2
         for half in range(2):
             value = piece(a, full[a], me, half)[...]
@@ -412,7 +416,7 @@
     drain(small_done.at[pl.ds(0, shares - 1)], done_sem.at[0])
     drain(squares_in.at[:, pl.ds(0, m - 1)], square_send)
     for a in range(4):
-        drain(unit_out[a], unit_send.at[a])
+        drain(unit_out[a], unit_sent[a])
     if turned:
         @pl.when(jnp.logical_or(me == 1, me == 2))
         def _():
@@ -426,12 +430,17 @@
 
 
 def finish(n, *refs):
-    results, full, own = refs[0:8], refs[8], refs[9]
-    outs, small_copies, small_news = refs[10:18], refs[18:20], refs[20:22]
-    copy_rows, new_rows, sem, small_sem = refs[22:24], refs[24:26], refs[26], refs[27]
-    moves = [pltpu.make_async_copy(results[i], outs[i], sem.at[i]) for i in range(8)]
+    copies, copy_mixed, news, new_mixed, full, own = refs[0:6]
+    outs, small_copies, small_news = refs[6:14], refs[14:16], refs[16:18]
+    copy_rows, new_rows, sem, small_sem = refs[18:20], refs[20:22], refs[22], refs[23]
+    for a in range(3):
+        pltpu.make_async_copy(copies.at[a], outs[a], sem.at[0]).start()
+    moves = [pltpu.make_async_copy(copy_mixed, outs[3], sem.at[1])]
+    moves.append(pltpu.make_async_copy(new_mixed, outs[7], sem.at[2]))
     for move in moves:
         move.start()
+    for a in range(3):
+        pltpu.make_async_copy(news.at[a], outs[4 + a], sem.at[3]).start()
     width = full.shape[-1]
     for i in range(2):
         for j in range(n):
@@ -440,8 +449,10 @@
     for i in range(2):
         moves.append(pltpu.make_async_copy(copy_rows[i], small_copies[i], small_sem.at[i]))
         moves.append(pltpu.make_async_copy(new_rows[i], small_news[i], small_sem.at[2 + i]))
-    for move in moves[8:]:
+    for move in moves[2:]:
         move.start()
+    drain(copies, sem.at[0])
+    drain(news, sem.at[3])
     for move in moves:
         move.wait()
 
@@ -473,11 +484,14 @@
             + [jax.ShapeDtypeStruct(b, f32) for b in blocks]
             + [jax.ShapeDtypeStruct((2, n, 1, width), f32), jax.ShapeDtypeStruct((2, 1, width), f32)]
         )
+        shapes = [o.shape for o in out_shape]
+        grouped = [((3,) + shapes[0], bf16), (shapes[3], bf16), ((3,) + shapes[4], f32), (shapes[7], f32)]
+        grouped += [(s, f32) for s in shapes[8:]]
         results = pl.pallas_call(
             functools.partial(kernel, n, m, n_x, n_y, turned),
-            out_shape=[pltpu.VMEM(o.shape, o.dtype) for o in out_shape],
+            out_shape=[pltpu.VMEM(s, t) for s, t in grouped],
             in_specs=[hbm] * 12,
-            out_specs=[vmem] * 10,
+            out_specs=[vmem] * 6,
             scratch_shapes=(
                 [pltpu.VMEM(g.shape[1:], f32) for g in grads]
                 + [pltpu.VMEM(b, f32) for b in blocks] * 2
@@ -499,7 +513,7 @@
                     DMA((4,)),
                     DMA,
                 ]
-                + [DMA((4,))] * 5
+                + [DMA, DMA((4,)), DMA((4,)), DMA((3,)), DMA((4,))]
                 + [DMA, DMA((4,)), DMA, DMA((2,)), DMA((3,))]
                 + [pltpu.SemaphoreType.REGULAR] * 2
             ),
@@ -512,11 +526,11 @@
             out_shape=out_shape[:8]
             + [jax.ShapeDtypeStruct((n * width,), bf16)] * 2
             + [jax.ShapeDtypeStruct((width,), f32)] * 2,
-            in_specs=[vmem] * 10,
+            in_specs=[vmem] * 6,
             out_specs=[hbm] * 12,
             scratch_shapes=[pltpu.VMEM((n * width,), bf16)] * 2
             + [pltpu.VMEM((width,), f32)] * 2
-            + [DMA((8,)), DMA((4,))],
+            + [DMA((4,)), DMA((4,))],
             compiler_params=pltpu.CompilerParams(vmem_limit_bytes=2**20),
         )(*results)
         return tuple(done[0:4]) + tuple(done[8:10]) + tuple(done[4:8]) + tuple(done[10:12])

time: 76.3 us -> 76.2 us (level)
  no operation moved by 1% of the time
where the time goes in v5:
time: 76.2 us; the launch traced here: 76.1 us
  Pallas kernels  75.4 us (99%)
    pallas_call x1, Pallas kernels, per_device(): pl.pallas_call(functools.partial(kernel, n, m, n_x, n_y, turned), out_sha...  72.7 us
    pallas_call x1, Pallas kernels, per_device(): pl.pallas_call(functools.partial(finish, n), out_shape=out_shape[:8] + [j...  2.74 us

profile of v5, /device:TPU:0, one launch (start us, length us, event | category | flops | bytes accessed | tf_op | source)
XLA Modules:
  0.0 76.1 jit_solution(5779266505934079844)
XLA Ops:
  0.6 72.7 %shard_map.211 = (bf16[3,2048,256]{2,1,0:T(8,128)(2,1)S(1)}, bf16[256,2048]{1,0:T(8,128)(2,1)S(1)}, f32[3,512,256]{2,1,0:T(8,128)S(1)}, f32[256,512]{1,0:T(8,128...) custom-call(f32[1,2048,256]{2,1,0:T(8,128)} %refs_0_.1, f32[1,2048,256]{2,1,0:T(8,128)} %refs_1_.1, ...), custom_call_target="tpu_custom_call" | custom-call | tf_op jit(solution)/shard_map/pallas_call | solution.py:490
  73.3 2.7 %shard_map.212 = (bf16[2048,256]{1,0:T(8,128)(2,1)}, bf16[2048,256]{1,0:T(8,128)(2,1)}, bf16[2048,256]{1,0:T(8,128)(2,1)}, bf16[256,2048]{1,0:T(8,128)(2,1)}, f3...) custom-call(bf16[3,2048,256]{2,1,0:T(8,128)(2,1)S(1)} %get-tuple-ele, ...), custom_call_target="tpu_custom_call" | custom-call | tf_op jit(solution)/shard_map/pallas_call | solution.py:524
